TPU v7x, 32 devices: a whole 2x2x4 slice. The times are simulated.
32 devices in a mesh: dp: 8 (over y, x, core), seq: 4 (over z).
Axes of the slice: x: 2, y: 2, z: 4, core: 2. Of those that a mesh axis runs over, the one named last changes fastest.
Arguments:
- query_rows: bfloat16 [8, 512, 3072], P('dp', 'seq'), may hold values from -6 to 6
- key_rows: bfloat16 [8, 512, 3072], P('dp', 'seq'), may hold values from -6 to 6
- value_rows: bfloat16 [8, 512, 3072], P('dp', 'seq'), may hold values from -6 to 6
- out_grad: bfloat16 [8, 512, 6144], P('dp', 'seq'), may hold values from -54 to 54
- clip_lengths: int32 [8, 4], P('dp'), may hold values from 1 to 256, 512 in all within a row
- out_weight: bfloat16 [3072, 6144], P('seq'), may hold values from -0.109375 to 0.109375
- query_gain: float32 [128], replicated, may hold values from 0.1 to 1.9
- key_gain: float32 [128], replicated, may hold values from 0.1 to 1.9
Outputs:
- query_grad: bfloat16 [8, 512, 3072], P('dp', 'seq')
- key_grad: bfloat16 [8, 512, 3072], P('dp', 'seq')
- value_grad: bfloat16 [8, 512, 3072], P('dp', 'seq')
- weight_grad: float32 [3072, 6144], P('seq', 'dp')
- querygain_grad: float32 [128], replicated
- keygain_grad: float32 [128], replicated
- grad_norm: float32 [], replicated
Inputs may be any that keep to these rules, and one draw needn't show every extreme that they name: `clip_lengths`: the token counts of each group's clips sum to 512.
All inputs are finite; a program needn't handle non-finite values.
Results may differ from a plain program's by a relative error of at most 0.015.
Values may be sent and summed in bfloat16 or wider, within the bound.
A program may use at most 128 MiB of HBM per device.

v0:
```python
import jax
import jax.numpy as jnp
from jax import lax
from jax.sharding import PartitionSpec as P

HEAD_DIM = 128
MAX_NORM = 768


EPS = 1e-06


def segment_ids(lengths, total):
    ends = jnp.cumsum(lengths)
    places = jnp.arange(total, dtype=jnp.int32)
    return jnp.sum((places[:, None] >= ends[None, :]).astype(jnp.int32), axis=1)


def norm_rows(rows, gain):
    wide = rows.astype(jnp.float32)
    inverse = lax.rsqrt(jnp.mean(wide * wide, axis=-1, keepdims=True) + EPS)
    unit = wide * inverse
    return (unit, inverse, (unit * gain).astype(jnp.bfloat16))


def norm_back(unit, inverse, gain, d_norm):
    gain_part = jnp.sum(unit * d_norm, axis=(0, 1))
    d_unit = d_norm * gain
    d_rows = inverse * (d_unit - unit * jnp.mean(unit * d_unit, axis=-1, keepdims=True))
    return (d_rows.astype(jnp.bfloat16), gain_part)


def local(
    query_rows, key_rows, value_rows, out_grad, clip_lengths, out_weight, query_gain, key_gain
):
    query, keys, values = (
        lax.all_to_all(query_rows[0], "seq", split_axis=1, concat_axis=0, tiled=True),
        lax.all_to_all(key_rows[0], "seq", split_axis=1, concat_axis=0, tiled=True),
        lax.all_to_all(value_rows[0], "seq", split_axis=1, concat_axis=0, tiled=True),
    )
    total = query.shape[0]
    heads = query.shape[1] // HEAD_DIM
    width = heads * HEAD_DIM
    scale = HEAD_DIM ** (-0.5)
    block = min(512, total)
    blocks = total // block
    seg = segment_ids(clip_lengths[0], total)
    q_unit, q_inv, q_norm = norm_rows(query.reshape(total, heads, HEAD_DIM), query_gain)
    k_unit, k_inv, k_norm = norm_rows(keys.reshape(total, heads, HEAD_DIM), key_gain)
    values3 = values.reshape(total, heads, HEAD_DIM)

    def forward_block(index):
        start = index * block
        query_block = lax.dynamic_slice_in_dim(q_norm, start, block, 0)
        seg_block = lax.dynamic_slice_in_dim(seg, start, block, 0)
        scores = (
            jnp.einsum("qhd,khd->hqk", query_block, k_norm, preferred_element_type=jnp.float32)
            * scale
        )
        same = seg_block[:, None] == seg[None, :]
        expo = jnp.where(same[None], jnp.exp(scores), 0.0)
        probs = (expo / jnp.sum(expo, axis=-1, keepdims=True)).astype(jnp.bfloat16)
        attn_out = jnp.einsum("hqk,khd->qhd", probs, values3, preferred_element_type=jnp.float32)
        return (probs, attn_out.astype(jnp.bfloat16))

    probs_all, attn_blocks = lax.map(forward_block, jnp.arange(blocks, dtype=jnp.int32))
    attn_flat = attn_blocks.reshape(total, width)
    out_full = lax.all_gather(out_grad[0], "seq", axis=0, tiled=True)
    weight_part = jnp.dot(attn_flat.T, out_full, preferred_element_type=jnp.float32)
    d_attn = jnp.dot(out_full, out_weight.T, preferred_element_type=jnp.float32).astype(
        jnp.bfloat16
    )
    d_attn3 = d_attn.reshape(total, heads, HEAD_DIM)

    def backward_block(carry, items):
        d_key, d_value = carry
        probs, index = items
        start = index * block
        attn_grad = lax.dynamic_slice_in_dim(d_attn3, start, block, 0)
        query_block = lax.dynamic_slice_in_dim(q_norm, start, block, 0)
        d_probs = jnp.einsum("qhd,khd->hqk", attn_grad, values3, preferred_element_type=jnp.float32)
        probs32 = probs.astype(jnp.float32)
        row_sum = jnp.sum(probs32 * d_probs, axis=-1, keepdims=True)
        d_scores = (probs32 * (d_probs - row_sum) * scale).astype(jnp.bfloat16)
        d_value = d_value + jnp.einsum(
            "hqk,qhd->khd", probs, attn_grad, preferred_element_type=jnp.float32
        )
        d_key = d_key + jnp.einsum(
            "hqk,qhd->khd", d_scores, query_block, preferred_element_type=jnp.float32
        )
        d_query = jnp.einsum("hqk,khd->qhd", d_scores, k_norm, preferred_element_type=jnp.float32)
        return ((d_key, d_value), d_query)

    empty = jnp.zeros((total, heads, HEAD_DIM), jnp.float32)
    (d_knorm, d_value32), d_query_blocks = lax.scan(
        backward_block, (empty, empty), (probs_all, jnp.arange(blocks, dtype=jnp.int32))
    )
    d_qnorm = d_query_blocks.reshape(total, heads, HEAD_DIM)
    query_grad, q_gain_part = norm_back(q_unit, q_inv, query_gain, d_qnorm)
    key_grad, k_gain_part = norm_back(k_unit, k_inv, key_gain, d_knorm)
    value_grad = d_value32.astype(jnp.bfloat16)
    query_back, key_back, value_back = (
        lax.all_to_all(
            query_grad.reshape(total, width), "seq", split_axis=0, concat_axis=1, tiled=True
        ),
        lax.all_to_all(
            key_grad.reshape(total, width), "seq", split_axis=0, concat_axis=1, tiled=True
        ),
        lax.all_to_all(
            value_grad.reshape(total, width), "seq", split_axis=0, concat_axis=1, tiled=True
        ),
    )
    weight_shard = lax.psum_scatter(
        weight_part.astype(jnp.bfloat16), "dp", scatter_dimension=1, tiled=True
    ).astype(jnp.float32)
    local_squares = jnp.sum(weight_shard * weight_shard)
    qgain_raw, kgain_raw = lax.psum((q_gain_part, k_gain_part), ("dp", "seq"))
    weight_squares = lax.psum(local_squares, ("dp", "seq"))
    squares = weight_squares + jnp.sum(qgain_raw * qgain_raw) + jnp.sum(kgain_raw * kgain_raw)
    grad_norm = jnp.sqrt(squares)
    factor = jnp.minimum(jnp.float32(1.0), MAX_NORM / (grad_norm + EPS))
    return (
        query_back[None],
        key_back[None],
        value_back[None],
        weight_shard * factor,
        qgain_raw * factor,
        kgain_raw * factor,
        grad_norm,
    )


def solution(mesh):
    placed = (
        P("dp", "seq", None),
        P("dp", "seq", None),
        P("dp", "seq", None),
        P("dp", "seq", None),
        P("dp", None),
        P("seq", None),
        P(),
        P(),
    )
    return jax.shard_map(
        local,
        mesh=mesh,
        in_specs=placed,
        out_specs=(
            P("dp", "seq", None),
            P("dp", "seq", None),
            P("dp", "seq", None),
            P("seq", "dp"),
            P(),
            P(),
            P(),
        ),
        check_vma=False,
    )
```

profile of v0, /device:TPU:12, one launch (start us, length us, event | category | flops | bytes accessed | tf_op | source)
XLA Modules:
  0.0 344.6 jit_solution(10818946303630261797)
XLA Ops:
  7.2 0.7 all-gather.3.cloned.1.call-update
  8.3 1.2 copy.65
  9.5 5.3 %all-to-all-start = ((bf16[128,4,768]{0,2,1:T(8,128)(2,1)}), bf16[128,4,768]{0,2,1:T(8,128)(2,1)S(1)}, u32[]{:S(2)}, u32[]{:S(2)}) async-start(bf16[128,4,768]{0,2,1:T(8,128)(2,1)} %bitcast), calls=%async_computation | async-start | bytes 1572864 | tf_op jit(solution)/shard_map/all_to_all | solution.py:37
  14.8 1.2 copy.67
  15.9 34.2 %all-to-all-done = bf16[128,4,768]{0,2,1:T(8,128)(2,1)S(1)} async-done(((bf16[128,4,768]{0,2,1:T(8,128)(2,1)}), bf16[128,4,768]{0,2,1:T(8,128)(2,1)S(1)}, u32[]{:S(2)}, u32[]{:S(2)}) %all-to-all-start) | async-done | bytes 786464 | tf_op jit(solution)/shard_map/all_to_all | solution.py:37
  50.1 8.0 %all-to-all-start.1 = ((bf16[128,4,768]{0,2,1:T(8,128)(2,1)}), bf16[128,4,768]{0,2,1:T(8,128)(2,1)S(1)}, u32[]{:S(2)}, u32[]{:S(2)}) async-start(bf16[128,4,768]{0,2,1:T(8,128)(2,1)} %bitcast.2), calls=%async_computation.1 | async-start | bytes 1572864 | tf_op jit(solution)/shard_map/all_to_all | solution.py:38
  58.2 1.2 copy.72
  59.3 36.6 %all-to-all-done.1 = bf16[128,4,768]{0,2,1:T(8,128)(2,1)S(1)} async-done(((bf16[128,4,768]{0,2,1:T(8,128)(2,1)}), bf16[128,4,768]{0,2,1:T(8,128)(2,1)S(1)}, u32[]{:S(2)}, u32[]{:S(2)}) %all-to-all-start.1) | async-done | bytes 786464 | tf_op jit(solution)/shard_map/all_to_all | solution.py:38
  96.0 6.1 %all-to-all-start.2 = ((bf16[128,4,768]{0,2,1:T(8,128)(2,1)}), bf16[128,4,768]{0,2,1:T(8,128)(2,1)}, u32[]{:S(2)}, u32[]{:S(2)}) async-start(bf16[128,4,768]{0,2,1:T(8,128)(2,1)} %bitcast.8), calls=%async_computation.2 | async-start | bytes 1572864 | tf_op jit(solution)/shard_map/all_to_all | solution.py:39
  102.6 1.0 copy.66
  103.7 0.6 reshape.151
  104.3 1.8 convert_bitcast_fusion
  106.1 2.2 copy.68
  108.3 1.9 reshape.152
  110.2 31.4 %all-to-all-done.2 = bf16[128,4,768]{0,2,1:T(8,128)(2,1)} async-done(((bf16[128,4,768]{0,2,1:T(8,128)(2,1)}), bf16[128,4,768]{0,2,1:T(8,128)(2,1)}, u32[]{:S(2)}, u32[]{:S(2)}) %all-to-all-start.2) | async-done | bytes 786464 | tf_op jit(solution)/shard_map/all_to_all | solution.py:39
  141.6 2.6 copy.73
  144.2 2.3 reshape.149
  147.2 1.9 fusion.6
  149.1 1.3 divide_convert_fusion
  150.5 1.5 convolution_convert_fusion.1
  151.9 14.7 %all-gather.3.cloned.1.call-done = bf16[1,512,6144]{2,1,0:T(8,128)(2,1)} async-done(((bf16[1,128,6144]{2,1,0:T(8,128)(2,1)}), bf16[1,512,6144]{2,1,0:T(8,128)(2,1)}) %all-gather.3.cloned.1.call-update) | async-done | bytes 6291472 | tf_op jit(solution)/shard_map/all_gather | solution.py:68
  166.6 9.6 %convolution_convert_fusion = bf16[768,6144]{1,0:T(8,128)(2,1)} fusion(bf16[512,768]{0,1:T(8,128)(2,1)} %bitcast.73, bf16[1,512,6144]{2,1,0:T(8,128)(2,1)} %all-gather.3.cloned.1.call-done), kind=kOutput, calls=%fused_computation.1 | convolution fusion | flops 4836556800 | bytes 16515072 | tf_op jit(solution)/shard_map/dot_general | solution.py:69
  176.2 10.7 %fusion.13 = bf16[512,768]{1,0:T(8,128)(2,1)} fusion(bf16[768,6144]{1,0:T(8,128)(2,1)} %param.13, bf16[1,512,6144]{2,1,0:T(8,128)(2,1)} %all-gather.3.cloned.1.call-done), kind=kOutput, calls=%fused_computation.36 | convolution fusion | flops 4832231424 | bytes 16515072 | tf_op jit(solution)/shard_map/dot_general | solution.py:70
  186.9 2.4 copy.71
  189.3 5.9 %fusion.22 = f32[6,512,512]{1,2,0:T(8,128)} fusion(bf16[512,6,128]{0,2,1:T(8,128)(2,1)} %bitcast.70, bf16[512,6,128]{0,2,1:T(8,128)(2,1)} %reshape.149), kind=kOutput, calls=%fused_computation.54 | convolution fusion | flops 402653184 | bytes 7864320 | tf_op jit(solution)/shard_map/while/body/eval_jaxpr/qhd,khd->hqk/dot_general | solution.py:81
  195.2 9.3 %fusion.12 = (f32[128]{0:T(128)S(1)}, f32[512,6]{0,1:T(8,128)S(1)}, f32[6,128,512]{2,1,0:T(8,128)}) fusion(f32[512,6,128]{0,2,1:T(8,128)} %copy-done, f32[512,6]{0,1:T(8,128)S(1)} %get-tuple-element.81, f32[128]{0:T(128)S(1)} %copy-done.8, bf16[6,512,512]{1,2,0:T(8,128)(2,1)S(1)} %divide_convert_fusion, f32[6,512,512]{1,2,0:T(8,128)} %fusion.22, ...), kind=kOutput, calls=%fused_computation.23 | convolution fusion | flops 417202560 | bytes 14194176 | tf_op jit(solution)/shard_map/while/body/eval_jaxpr/hqk,khd->qhd/dot_general | solution.py:91
  204.6 3.7 %multiply_convert_fusion.1 = bf16[512,6,128]{0,2,1:T(8,128)(2,1)} fusion(f32[6,128,512]{2,1,0:T(8,128)} %get-tuple-element.78, f32[512,6,128]{0,2,1:T(8,128)} %copy-done, f32[512,6]{0,1:T(8,128)S(1)} %broadcast_multiply_fusion.1, f32[128]{0:T(128)S(1)} %copy-done.8, f32[512,6]{0,1:T(8,128)S(1)} %get-tuple-element.81), kind=kLoop, calls=%fused_computation.28 | loop fusion | flops 2359296 | bytes 3957248 | tf_op jit(solution)/shard_map/convert_element_type | solution.py:30
  208.2 2.4 all_to_all.75
  210.7 2.2 copy.77
  212.8 6.5 %all-to-all-start.3 = ((bf16[4,128,768]{1,2,0:T(8,128)(2,1)}), bf16[4,128,768]{1,2,0:T(8,128)(2,1)}, u32[]{:S(2)}, u32[]{:S(2)}) async-start(bf16[4,128,768]{1,2,0:T(8,128)(2,1)} %copy.77), calls=%async_computation.3 | async-start | bytes 1572864 | tf_op jit(solution)/shard_map/all_to_all | solution.py:103
  219.4 9.8 %fusion.11 = (f32[128]{0:T(128)S(1)}, f32[512,6]{0,1:T(8,128)S(1)}, f32[6,128,512]{2,1,0:T(8,128)}) fusion(f32[512,6,128]{0,2,1:T(8,128)} %copy-done.1, f32[512,6]{0,1:T(8,128)S(1)} %get-tuple-element.80, f32[128]{0:T(128)S(1)} %copy-done.9, bf16[6,512,512]{1,2,0:T(8,128)(2,1)S(1)} %divide_convert_fusion, f32[6,512,512]{1,2,0:T(8,128)} %fusion.22, ...), kind=kOutput, calls=%fused_computation.20 | convolution fusion | flops 417202560 | bytes 14194176 | tf_op jit(solution)/shard_map/while/body/eval_jaxpr/hqk,qhd->khd/dot_general | solution.py:88
  229.2 3.3 multiply_convert_fusion
  232.5 2.5 all_to_all.78
  234.9 2.1 copy.79
  237.0 7.2 %all-to-all-start.4 = ((bf16[4,128,768]{1,2,0:T(8,128)(2,1)}), bf16[4,128,768]{1,2,0:T(8,128)(2,1)}, u32[]{:S(2)}, u32[]{:S(2)}) async-start(bf16[4,128,768]{1,2,0:T(8,128)(2,1)} %copy.79), calls=%async_computation.4 | async-start | bytes 1572864 | tf_op jit(solution)/shard_map/all_to_all | solution.py:106
  244.3 3.2 fusion.16
  247.4 1.7 all_to_all.81
  249.2 1.0 copy.81
  250.2 10.6 %all-to-all-done.4 = bf16[4,128,768]{1,2,0:T(8,128)(2,1)} async-done(((bf16[4,128,768]{1,2,0:T(8,128)(2,1)}), bf16[4,128,768]{1,2,0:T(8,128)(2,1)}, u32[]{:S(2)}, u32[]{:S(2)}) %all-to-all-start.4) | async-done | bytes 786464 | tf_op jit(solution)/shard_map/all_to_all | solution.py:106
  260.7 6.8 %all-to-all-start.5 = ((bf16[4,128,768]{1,2,0:T(8,128)(2,1)}), bf16[4,128,768]{1,2,0:T(8,128)(2,1)S(1)}, u32[]{:S(2)}, u32[]{:S(2)}) async-start(bf16[4,128,768]{1,2,0:T(8,128)(2,1)} %copy.81), calls=%async_computation.5 | async-start | bytes 1572864 | tf_op jit(solution)/shard_map/all_to_all | solution.py:109
  267.6 2.3 copy.83
  269.9 2.3 copy.84
  272.2 11.8 %all-to-all-done.5 = bf16[4,128,768]{1,2,0:T(8,128)(2,1)S(1)} async-done(((bf16[4,128,768]{1,2,0:T(8,128)(2,1)}), bf16[4,128,768]{1,2,0:T(8,128)(2,1)S(1)}, u32[]{:S(2)}, u32[]{:S(2)}) %all-to-all-start.5) | async-done | bytes 786464 | tf_op jit(solution)/shard_map/all_to_all | solution.py:109
  284.0 1.2 copy.85
  285.2 2.6 fusion.10
  287.7 43.1 %all-reduce = (f32[]{:T(128)}, f32[128]{0:T(128)S(1)}, f32[128]{0:T(128)S(1)}) all-reduce(f32[]{:T(128)} %fusion.10, f32[128]{0:T(128)S(1)} %get-tuple-element.71, f32[128]{0:T(128)S(1)} %get-tuple-element.69), channel_id=1, replica_groups=mesh['dp'=8,'seq'=4] {'dp','seq'}, use_global_device_ids=true, to_apply=%region_10.11 | all-reduce | flops 257 | bytes 2056 | tf_op jit(solution)/shard_map/psum | solution.py:118
  330.8 0.6 multiply_reduce_fusion.5
  335.1 1.6 convert_multiply_fusion.9
  (39 shorter events, 3.3 us)
Async XLA Ops:
  7.2 1.1 copy-start.5
  7.2 159.5 %all-gather.3.cloned.1.call-start = ((), (), s32[]{:S(2)}) async-start(), calls=%async_computation.8 | async-start | bytes 7864320 | tf_op jit(solution)/shard_map/all_gather | solution.py:68
  8.3 6.5 %copy-start.6 = (bf16[1,128,3072]{2,1,0:T(8,128)(2,1)S(1)}, bf16[1,128,3072]{2,1,0:T(8,128)(2,1)}, u32[]{:S(2)}) copy-start(bf16[1,128,3072]{2,1,0:T(8,128)(2,1)} %param.9) | copy-start | bytes 2359300
  9.5 40.7 %all-to-all-start = ((bf16[128,4,768]{0,2,1:T(8,128)(2,1)}), bf16[128,4,768]{0,2,1:T(8,128)(2,1)S(1)}, u32[]{:S(2)}, u32[]{:S(2)}) async-start(bf16[128,4,768]{0,2,1:T(8,128)(2,1)} %bitcast), calls=%async_computation | async-start | bytes 1572864 | tf_op jit(solution)/shard_map/all_to_all | solution.py:37
  14.8 43.4 %copy-start.7 = (bf16[1,128,3072]{2,1,0:T(8,128)(2,1)S(1)}, bf16[1,128,3072]{2,1,0:T(8,128)(2,1)}, u32[]{:S(2)}) copy-start(bf16[1,128,3072]{2,1,0:T(8,128)(2,1)} %param.10) | copy-start | bytes 2359300
  50.1 45.8 %all-to-all-start.1 = ((bf16[128,4,768]{0,2,1:T(8,128)(2,1)}), bf16[128,4,768]{0,2,1:T(8,128)(2,1)S(1)}, u32[]{:S(2)}, u32[]{:S(2)}) async-start(bf16[128,4,768]{0,2,1:T(8,128)(2,1)} %bitcast.2), calls=%async_computation.1 | async-start | bytes 1572864 | tf_op jit(solution)/shard_map/all_to_all | solution.py:38
  58.2 43.9 %copy-start.10 = (s32[1,4]{1,0:T(1,128)S(1)}, s32[1,4]{1,0:T(1,128)}, u32[]{:S(2)}) copy-start(s32[1,4]{1,0:T(1,128)} %param.12) | copy-start | bytes 52
  96.0 6.7 %copy-start.4 = (bf16[128,4,768]{0,2,1:T(8,128)(2,1)}, bf16[128,4,768]{0,2,1:T(8,128)(2,1)S(1)}, u32[]{:S(2)}) copy-start(bf16[128,4,768]{0,2,1:T(8,128)(2,1)S(1)} %all-to-all-done.1) | copy-start | bytes 2359300
  96.0 45.6 %all-to-all-start.2 = ((bf16[128,4,768]{0,2,1:T(8,128)(2,1)}), bf16[128,4,768]{0,2,1:T(8,128)(2,1)}, u32[]{:S(2)}, u32[]{:S(2)}) async-start(bf16[128,4,768]{0,2,1:T(8,128)(2,1)} %bitcast.8), calls=%async_computation.2 | async-start | bytes 1572864 | tf_op jit(solution)/shard_map/all_to_all | solution.py:39
  102.0 183.1 %reduce-scatter.2.cloned.1.call-start = ((), (), s32[]{:S(2)}) async-start(), calls=%async_computation.7 | async-start | bytes 10616832 | tf_op jit(solution)/shard_map/reduce_scatter | solution.py:113
  104.3 42.7 %copy-start = (f32[512,6,128]{0,2,1:T(8,128)}, f32[512,6,128]{0,2,1:T(8,128)S(1)}, u32[]{:S(2)}) copy-start(f32[512,6,128]{0,2,1:T(8,128)S(1)} %reshape.151) | copy-start | bytes 4718596
  110.2 36.8 %copy-start.1 = (f32[512,6,128]{0,2,1:T(8,128)}, f32[512,6,128]{0,2,1:T(8,128)S(1)}, u32[]{:S(2)}) copy-start(f32[512,6,128]{0,2,1:T(8,128)S(1)} %reshape.152) | copy-start | bytes 4718596
  146.6 0.7 copy-start.8
  146.6 0.7 copy-start.9
  149.1 1.3 copy-start.2
  212.8 24.2 %all-to-all-start.3 = ((bf16[4,128,768]{1,2,0:T(8,128)(2,1)}), bf16[4,128,768]{1,2,0:T(8,128)(2,1)}, u32[]{:S(2)}, u32[]{:S(2)}) async-start(bf16[4,128,768]{1,2,0:T(8,128)(2,1)} %copy.77), calls=%async_computation.3 | async-start | bytes 1572864 | tf_op jit(solution)/shard_map/all_to_all | solution.py:103
  237.0 23.7 %all-to-all-start.4 = ((bf16[4,128,768]{1,2,0:T(8,128)(2,1)}), bf16[4,128,768]{1,2,0:T(8,128)(2,1)}, u32[]{:S(2)}, u32[]{:S(2)}) async-start(bf16[4,128,768]{1,2,0:T(8,128)(2,1)} %copy.79), calls=%async_computation.4 | async-start | bytes 1572864 | tf_op jit(solution)/shard_map/all_to_all | solution.py:106
  260.7 23.2 %all-to-all-start.5 = ((bf16[4,128,768]{1,2,0:T(8,128)(2,1)}), bf16[4,128,768]{1,2,0:T(8,128)(2,1)S(1)}, u32[]{:S(2)}, u32[]{:S(2)}) async-start(bf16[4,128,768]{1,2,0:T(8,128)(2,1)} %copy.81), calls=%async_computation.5 | async-start | bytes 1572864 | tf_op jit(solution)/shard_map/all_to_all | solution.py:109
  285.1 49.9 %copy-start.3 = (bf16[768,768]{1,0:T(8,128)(2,1)S(1)}, bf16[768,768]{1,0:T(8,128)(2,1)}, u32[]{:S(2)}) copy-start(bf16[768,768]{1,0:T(8,128)(2,1)} %reduce-scatter.2.cloned.1.call-done) | copy-start | bytes 3538948
Sparse Core Ops, SparseCore 0:
  9.6 157.0 all-gather.2
  176.3 78.6 reduce-scatter.1
where the time goes:
time: 346 us; the launch traced here: 345 us
  waiting for transfers between devices  140 us (40%)
  matrix products  51.8 us (15%)
  blocking collectives  43.1 us (12%)
  starting transfers between devices  40 us (12%)
  local copies, waits for them, and re-layouts  34.8 us (10%)
  other arithmetic  17.4 us (5%)
  between operations  17.4 us (5%)
    psum x1, blocking collectives, local(): weight_squares = lax.psum(local_squares, ('dp', 'seq'))  43.1 us
    all_to_all x1, waiting for transfers between devices, local(): lax.all_to_all(key_rows[0], 'seq', split_axis=1, concat_axis=0, tiled=True)  36.6 us
    all_to_all x1, waiting for transfers between devices, local(): lax.all_to_all(query_rows[0], 'seq', split_axis=1, concat_axis=0, tiled=T...  34.2 us
    all_to_all x1, waiting for transfers between devices, local(): lax.all_to_all(value_rows[0], 'seq', split_axis=1, concat_axis=0, tiled=T...  31.4 us
    all_gather x1, waiting for transfers between devices, local(): out_full = lax.all_gather(out_grad[0], 'seq', axis=0, tiled=True)  14.7 us
    all_to_all x1, waiting for transfers between devices, local(): lax.all_to_all(value_grad.reshape(total, width), 'seq', split_axis=0, con...  11.8 us
    dot_general x1, matrix products, local(): jnp.dot(out_full, out_weight.T, preferred_element_type=jnp.float32)  10.7 us
    all_to_all x1, waiting for transfers between devices, local(): lax.all_to_all(key_grad.reshape(total, width), 'seq', split_axis=0, conca...  10.6 us
  transfers between devices with their start and end apart: 8, of which 6 were waited for; matrix products, arithmetic and copies ran while one was open for 23% of the time, Pallas kernels for 0%

commit v1 on v0

v1 whole, which is shorter than its diff:
```python
import functools

import jax
import jax.numpy as jnp
from jax import lax
from jax.experimental import pallas as pl
from jax.experimental.pallas import tpu as pltpu
from jax.sharding import PartitionSpec as P

HEAD_DIM = 128
MAX_NORM = 768
EPS = 1e-06
CHUNKS = 4
SCALE = HEAD_DIM ** (-0.5)
NT = (((1,), (1,)), ((), ()))
TN = (((0,), (0,)), ((), ()))
NN = (((1,), (0,)), ((), ()))


def mm(a, b, dims):
    return lax.dot_general(a, b, dims, preferred_element_type=jnp.float32)


def segment_ids(lengths, total):
    ends = jnp.cumsum(lengths)
    places = jnp.arange(total, dtype=jnp.int32)
    return jnp.sum((places[:, None] >= ends[None, :]).astype(jnp.int32), axis=1)


def unit_rows(rows):
    wide = rows.astype(jnp.float32)
    inverse = lax.rsqrt(jnp.mean(wide * wide, axis=-1, keepdims=True) + EPS)
    return wide * inverse, inverse


def probs_of(qn, kn, same):
    scores = mm(qn, kn, NT) * SCALE
    expo = jnp.where(same, jnp.exp(scores), 0.0)
    return (expo * (1.0 / jnp.sum(expo, axis=-1, keepdims=True))).astype(jnp.bfloat16)


def forward_kernel(qkv_ref, row_ref, col_ref, qg_ref, kg_ref, out_ref):
    n, _, rows, _ = qkv_ref.shape
    total = n * rows
    q = qkv_ref[:, 0].reshape(total, HEAD_DIM)
    k = qkv_ref[:, 1].reshape(total, HEAD_DIM)
    v = qkv_ref[:, 2].reshape(total, HEAD_DIM)
    qn = (unit_rows(q)[0] * qg_ref[...]).astype(jnp.bfloat16)
    kn = (unit_rows(k)[0] * kg_ref[...]).astype(jnp.bfloat16)
    same = row_ref[...] == col_ref[...]
    probs = probs_of(qn, kn, same)
    out = mm(probs, v, NN).astype(jnp.bfloat16)
    out_ref[...] = out.reshape(n, rows, HEAD_DIM)


def norm_back(unit, inverse, gain, d_norm):
    part = jnp.sum(unit * d_norm, axis=0, keepdims=True)
    d_unit = d_norm * gain
    d_rows = inverse * (d_unit - unit * jnp.mean(unit * d_unit, axis=-1, keepdims=True))
    return d_rows.astype(jnp.bfloat16), part


def backward_kernel(qkv_ref, row_ref, col_ref, qg_ref, kg_ref, *refs):
    d_refs, (grad_ref, qpart_ref, kpart_ref) = refs[:-3], refs[-3:]
    n, _, rows, _ = qkv_ref.shape
    total = n * rows
    q = qkv_ref[:, 0].reshape(total, HEAD_DIM)
    k = qkv_ref[:, 1].reshape(total, HEAD_DIM)
    v = qkv_ref[:, 2].reshape(total, HEAD_DIM)
    q_unit, q_inv = unit_rows(q)
    k_unit, k_inv = unit_rows(k)
    qg, kg = qg_ref[...], kg_ref[...]
    qn = (q_unit * qg).astype(jnp.bfloat16)
    kn = (k_unit * kg).astype(jnp.bfloat16)
    probs = probs_of(qn, kn, row_ref[...] == col_ref[...])
    pieces = []
    for ref in d_refs:
        piece = ref[0].astype(jnp.float32)
        for source in range(1, ref.shape[0]):
            piece = piece + ref[source].astype(jnp.float32)
        pieces.append(piece)
    d_attn = jnp.concatenate(pieces, axis=1).reshape(total, HEAD_DIM).astype(jnp.bfloat16)
    d_probs = mm(d_attn, v, NT)
    probs32 = probs.astype(jnp.float32)
    row_sum = jnp.sum(probs32 * d_probs, axis=-1, keepdims=True)
    d_scores = (probs32 * (d_probs - row_sum) * SCALE).astype(jnp.bfloat16)
    d_value = mm(probs, d_attn, TN).astype(jnp.bfloat16)
    d_query, qpart = norm_back(q_unit, q_inv, qg, mm(d_scores, kn, NN))
    d_key, kpart = norm_back(k_unit, k_inv, kg, mm(d_scores, qn, TN))
    grad_ref[:, 0] = d_query.reshape(n, rows, HEAD_DIM)
    grad_ref[:, 1] = d_key.reshape(n, rows, HEAD_DIM)
    grad_ref[:, 2] = d_value.reshape(n, rows, HEAD_DIM)

    @pl.when(pl.program_id(0) == 0)
    def _():
        qpart_ref[...] = jnp.zeros_like(qpart_ref)
        kpart_ref[...] = jnp.zeros_like(kpart_ref)

    qpart_ref[...] += qpart
    kpart_ref[...] += kpart


def local(
    query_rows, key_rows, value_rows, out_grad, clip_lengths, out_weight, query_gain, key_gain,
    n, groups,
):
    rows, inner = query_rows.shape[1:]
    width = inner // n
    heads = width // HEAD_DIM
    total = n * rows
    columns = out_grad.shape[2] // groups
    piece = rows // CHUNKS

    parts = out_grad[0].reshape(rows, groups, columns).transpose(1, 0, 2)
    parts = lax.all_to_all(parts, "dp", split_axis=0, concat_axis=0, tiled=True)
    qkv = jnp.stack([query_rows[0], key_rows[0], value_rows[0]])
    qkv = qkv.reshape(3, rows, n, width).transpose(2, 0, 1, 3)
    qkv = lax.all_to_all(qkv, "seq", split_axis=0, concat_axis=0, tiled=True)

    seg = segment_ids(clip_lengths[0], total)
    seg_row, seg_col = seg[:, None], seg[None, :]
    qg, kg = query_gain[None], key_gain[None]
    qkv_spec = pl.BlockSpec((n, 3, rows, HEAD_DIM), lambda h: (0, 0, 0, h))
    small = [
        pl.BlockSpec((total, 1), lambda h: (0, 0)),
        pl.BlockSpec((1, total), lambda h: (0, 0)),
        pl.BlockSpec((1, HEAD_DIM), lambda h: (0, 0)),
        pl.BlockSpec((1, HEAD_DIM), lambda h: (0, 0)),
    ]
    params = pltpu.CompilerParams(
        dimension_semantics=("arbitrary",), vmem_limit_bytes=60 * 1024 * 1024
    )
    square = total * total * heads
    attn = pl.pallas_call(
        forward_kernel,
        grid=(heads,),
        in_specs=[qkv_spec] + small,
        out_specs=pl.BlockSpec((n, rows, HEAD_DIM), lambda h: (0, 0, h)),
        out_shape=jax.ShapeDtypeStruct((n, rows, width), jnp.bfloat16),
        compiler_params=params,
        cost_estimate=pl.CostEstimate(
            flops=4 * square * HEAD_DIM, bytes_accessed=8 * total * width, transcendentals=square
        ),
        name="forward",
    )(qkv, seg_row, seg_col, qg, kg)
    attn_all = lax.all_to_all(
        jnp.broadcast_to(attn[None], (groups,) + attn.shape),
        "dp", split_axis=0, concat_axis=0, tiled=True,
    )

    start = lax.axis_index("dp") * columns
    weight = lax.dynamic_slice_in_dim(out_weight, start, columns, 1)
    weight_raw = jnp.zeros((width, columns), jnp.float32)
    d_parts = []
    for j in range(CHUNKS):
        mine = lax.slice_in_dim(parts, j * piece, (j + 1) * piece, axis=1)
        full = lax.all_gather(mine, "seq", axis=1)
        partial = jnp.einsum(
            "gtrc,hc->gtrh", full, weight, preferred_element_type=jnp.float32
        ).astype(jnp.bfloat16)
        d_parts.append(lax.all_to_all(partial, "dp", split_axis=0, concat_axis=0, tiled=True))
        slab = lax.slice_in_dim(attn_all, j * piece, (j + 1) * piece, axis=2)
        weight_raw = weight_raw + jnp.einsum(
            "gtrh,gtrc->hc", slab, full, preferred_element_type=jnp.float32
        )

    d_spec = pl.BlockSpec((groups, n, piece, HEAD_DIM), lambda h: (0, 0, 0, h))
    one = pl.BlockSpec((1, HEAD_DIM), lambda h: (0, 0))
    row = jax.ShapeDtypeStruct((1, HEAD_DIM), jnp.float32)
    grads, qpart, kpart = pl.pallas_call(
        backward_kernel,
        grid=(heads,),
        in_specs=[qkv_spec] + small + [d_spec] * CHUNKS,
        out_specs=(qkv_spec, one, one),
        out_shape=(jax.ShapeDtypeStruct((n, 3, rows, width), jnp.bfloat16), row, row),
        compiler_params=params,
        cost_estimate=pl.CostEstimate(
            flops=12 * square * HEAD_DIM, bytes_accessed=28 * total * width, transcendentals=square
        ),
        name="backward",
    )(qkv, seg_row, seg_col, qg, kg, *d_parts)
    back = lax.all_to_all(grads, "seq", split_axis=0, concat_axis=0, tiled=True)
    query_back, key_back, value_back = (
        back[:, i].transpose(1, 0, 2).reshape(1, rows, inner) for i in range(3)
    )

    packed = jnp.concatenate(
        [qpart[0], kpart[0], jnp.full((HEAD_DIM,), jnp.sum(weight_raw * weight_raw))]
    )
    packed = lax.psum(packed, ("dp", "seq"))
    qgain_raw, kgain_raw = packed[:HEAD_DIM], packed[HEAD_DIM : 2 * HEAD_DIM]
    squares = (
        packed[2 * HEAD_DIM] + jnp.sum(qgain_raw * qgain_raw) + jnp.sum(kgain_raw * kgain_raw)
    )
    grad_norm = jnp.sqrt(squares)
    factor = jnp.minimum(jnp.float32(1.0), MAX_NORM / (grad_norm + EPS))
    return (
        query_back,
        key_back,
        value_back,
        weight_raw * factor,
        qgain_raw * factor,
        kgain_raw * factor,
        grad_norm,
    )


def solution(mesh):
    rows = P("dp", "seq", None)
    return jax.shard_map(
        functools.partial(local, n=mesh.shape["seq"], groups=mesh.shape["dp"]),
        mesh=mesh,
        in_specs=(rows, rows, rows, rows, P("dp", None), P("seq", None), P(), P()),
        out_specs=(rows, rows, rows, P("seq", "dp"), P(), P(), P()),
        check_vma=False,
    )
```

time: 346 us -> 469 us (1.36)
  waiting for transfers between devices: 140 us -> 267 us
  blocking collectives: 43.1 us -> 65.6 us
  matrix products: 51.8 us -> 30.3 us
  Pallas kernels: 0 us -> 21 us
  other arithmetic: 17.4 us -> 4.58 us
  local copies, waits for them, and re-layouts: 34.8 us -> 27.8 us
  starting transfers between devices: 40 us -> 34.8 us
    all_to_all x6 -> x7, waiting for transfers between devices: 125 us -> 191 us  [the longest x1 63.7 us: local(): lax.all_to_all(jnp.broadcast_to(attn[None], (groups,) + attn.shape), 'dp'...]
    all_gather x1 -> x4, waiting for transfers between devices: 14.7 us -> 73.5 us  [local(): full = lax.all_gather(mine, 'seq', axis=1)]
    all_to_all x0 -> x1, blocking collectives: none -> 23.5 us  [local(): parts = lax.all_to_all(parts, 'dp', split_axis=0, concat_axis=0, tiled=True)]
    dot_general x8, matrix products: 51.8 us -> 30.3 us  [the longest x4 17.5 us: local(): jnp.einsum('gtrc,hc->gtrh', full, weight, preferred_element_type=jnp.floa...]
    pallas_call x0 -> x2, Pallas kernels: none -> 21 us  [the longest x1 12.4 us: local(): pl.pallas_call(backward_kernel, grid=(heads,), in_specs=[qkv_spec] + smal...]
    all_to_all x7 -> x0, local copies, waits for them, and re-layouts: 14.5 us -> none  [the longest x2 4.6 us: local(): lax.all_to_all(query_grad.reshape(total, width), 'seq', split_axis=0, con...]
    convert_element_type x5 -> x0, other arithmetic: 10.2 us -> none  [the longest x2 6.95 us: norm_back(): return (d_rows.astype(jnp.bfloat16), gain_part)]
    convert_element_type x5 -> x0, local copies, waits for them, and re-layouts: 8.13 us -> none  [the longest x4 5.72 us: norm_rows(): wide = rows.astype(jnp.float32)]
  transfers between devices with their start and end apart: 8 -> 11, of which waited for: 6 -> 9; matrix products, arithmetic and copies ran while one was open for 23% -> 7% of each run, Pallas kernels for 0% -> 2%
where the time goes in v1:
time: 469 us; the launch traced here: 468 us
  waiting for transfers between devices  267 us (57%)
  blocking collectives  65.6 us (14%)
  starting transfers between devices  34.8 us (7%)
  matrix products  30.3 us (6%)
  local copies, waits for them, and re-layouts  27.8 us (6%)
  Pallas kernels  21 us (4%)
  between operations  17.1 us (4%)
    all_gather x4, waiting for transfers between devices, local(): full = lax.all_gather(mine, 'seq', axis=1)  73.5 us
    all_to_all x1, waiting for transfers between devices, local(): lax.all_to_all(jnp.broadcast_to(attn[None], (groups,) + attn.shape), 'dp'...  63.7 us
    all_to_all x1, waiting for transfers between devices, local(): qkv = lax.all_to_all(qkv, 'seq', split_axis=0, concat_axis=0, tiled=True)  47.6 us
    psum x1, blocking collectives, local(): packed = lax.psum(packed, ('dp', 'seq'))  42 us
    all_to_all x1, waiting for transfers between devices, local(): back = lax.all_to_all(grads, 'seq', split_axis=0, concat_axis=0, tiled=True)  40.1 us
    all_to_all x4, waiting for transfers between devices, local(): lax.all_to_all(partial, 'dp', split_axis=0, concat_axis=0, tiled=True)  39.7 us
    all_to_all x1, blocking collectives, local(): parts = lax.all_to_all(parts, 'dp', split_axis=0, concat_axis=0, tiled=True)  23.5 us
    all_to_all x4, starting transfers between devices, local(): lax.all_to_all(partial, 'dp', split_axis=0, concat_axis=0, tiled=True)  18.8 us
  transfers between devices with their start and end apart: 11, of which 9 were waited for; matrix products, arithmetic and copies ran while one was open for 7% of the time, Pallas kernels for 2%

profile of v1, /device:TPU:12, one launch (start us, length us, event | category | flops | bytes accessed | tf_op | source)
XLA Modules:
  0.0 467.7 jit_solution(10691603811483705762)
XLA Ops:
  7.2 1.7 copy.47
  9.3 23.5 %all_to_all.40 = bf16[8,128,768]{2,1,0:T(8,128)(2,1)S(1)} all-to-all(bf16[8,128,768]{2,1,0:T(8,128)(2,1)S(1)} %bitcast.85), channel_id=1, replica_groups=mesh['dp'=8,'seq'=4] {'dp'}, dimensions={0} | all-to-all | bytes 3145728 | tf_op jit(solution)/shard_map/all_to_all | solution.py:115
  32.8 1.2 fusion.23
  35.1 1.2 copy.30
  36.3 1.2 copy.31
  37.5 1.6 pad_maximum_fusion
  39.1 2.4 copy.32
  41.5 5.3 %all-to-all-start = ((bf16[4,3,128,768]{3,2,1,0:T(8,128)(2,1)}), bf16[4,3,128,768]{3,2,1,0:T(8,128)(2,1)S(1)}, u32[]{:S(2)}, u32[]{:S(2)}) async-start(bf16[4,3,128,768]{3,2,1,0:T(8,128)(2,1)} %bitcast.83), calls=%async_computation | async-start | bytes 4718592 | tf_op jit(solution)/shard_map/all_to_all | solution.py:118
  46.8 0.7 all-gather.11.cloned.1.call-update
  47.6 0.7 all-gather.13.cloned.1.call-update
  48.3 43.7 %all-gather.9.cloned.1.call-done = bf16[8,128,768]{2,1,0:T(8,128)(2,1)} async-done(((bf16[8,32,768]{2,1,0:T(8,128)(2,1)}), bf16[8,128,768]{2,1,0:T(8,128)(2,1)}) %all-gather.9.cloned.1.call-update) | async-done | bytes 1572880 | tf_op jit(solution)/shard_map/all_gather | solution.py:157
  92.0 4.4 fusion.7
  96.4 47.6 %all-to-all-done.qkv_ref = bf16[4,3,128,768]{3,2,1,0:T(8,128)(2,1)S(1)} async-done(((bf16[4,3,128,768]{3,2,1,0:T(8,128)(2,1)}), bf16[4,3,128,768]{3,2,1,0:T(8,128)(2,1)S(1)}, u32[]{:S(2)}, u32[]{:S(2)}) %all-to-all-start) | async-done | bytes 2359328 | tf_op jit(solution)/shard_map/all_to_all | solution.py:118
  144.1 1.4 copy-done
  145.5 4.6 all-to-all-start.2
  150.1 4.4 fusion.8
  154.5 15.2 %all-to-all-done.2.refs_0_ = bf16[8,4,32,768]{3,2,1,0:T(8,128)(2,1)} async-done(((bf16[8,4,32,768]{3,2,1,0:T(8,128)(2,1)}), bf16[8,4,32,768]{3,2,1,0:T(8,128)(2,1)}, u32[]{:S(2)}, u32[]{:S(2)}) %all-to-all-start.2) | async-done | bytes 1572896 | tf_op jit(solution)/shard_map/all_to_all | solution.py:161
  169.7 5.0 %all-to-all-start.3 = ((bf16[8,4,32,768]{3,2,1,0:T(8,128)(2,1)}), bf16[8,4,32,768]{3,2,1,0:T(8,128)(2,1)S(1)}, u32[]{:S(2)}, u32[]{:S(2)}) async-start(bf16[8,4,32,768]{3,2,1,0:T(8,128)(2,1)} %fusion.8), calls=%async_computation.3 | async-start | bytes 3145728 | tf_op jit(solution)/shard_map/all_to_all | solution.py:161
  175.2 8.5 %all-gather.13.cloned.1.call-done = bf16[8,128,768]{2,1,0:T(8,128)(2,1)} async-done(((bf16[8,32,768]{2,1,0:T(8,128)(2,1)}), bf16[8,128,768]{2,1,0:T(8,128)(2,1)}) %all-gather.13.cloned.1.call-update) | async-done | bytes 1572880 | tf_op jit(solution)/shard_map/all_gather | solution.py:157
  183.8 4.4 fusion.9
  188.1 6.1 %all-to-all-done.3.refs_1_ = bf16[8,4,32,768]{3,2,1,0:T(8,128)(2,1)S(1)} async-done(((bf16[8,4,32,768]{3,2,1,0:T(8,128)(2,1)}), bf16[8,4,32,768]{3,2,1,0:T(8,128)(2,1)S(1)}, u32[]{:S(2)}, u32[]{:S(2)}) %all-to-all-start.3) | async-done | bytes 1572896 | tf_op jit(solution)/shard_map/all_to_all | solution.py:161
  194.2 1.2 copy-done.2
  195.4 5.0 %all-to-all-start.4 = ((bf16[8,4,32,768]{3,2,1,0:T(8,128)(2,1)}), bf16[8,4,32,768]{3,2,1,0:T(8,128)(2,1)S(1)}, u32[]{:S(2)}, u32[]{:S(2)}) async-start(bf16[8,4,32,768]{3,2,1,0:T(8,128)(2,1)} %fusion.9), calls=%async_computation.4 | async-start | bytes 3145728 | tf_op jit(solution)/shard_map/all_to_all | solution.py:161
  200.4 21.3 %all-gather.15.cloned.1.call-done = bf16[8,128,768]{2,1,0:T(8,128)(2,1)} async-done(((bf16[8,32,768]{2,1,0:T(8,128)(2,1)}), bf16[8,128,768]{2,1,0:T(8,128)(2,1)}) %all-gather.15.cloned.1.call-update) | async-done | bytes 1572880 | tf_op jit(solution)/shard_map/all_gather | solution.py:157
  221.7 4.4 fusion.10
  226.1 1.2 copy-done.3
  227.3 4.2 all-to-all-start.5
  231.7 0.9 copy.34.row_ref
  232.6 18.4 %all-to-all-done.5.refs_3_ = bf16[8,4,32,768]{3,2,1,0:T(8,128)(2,1)S(1)} async-done(((bf16[8,4,32,768]{3,2,1,0:T(8,128)(2,1)}), bf16[8,4,32,768]{3,2,1,0:T(8,128)(2,1)S(1)}, u32[]{:S(2)}, u32[]{:S(2)}) %all-to-all-start.5) | async-done | bytes 1572896 | tf_op jit(solution)/shard_map/all_to_all | solution.py:161
  251.0 1.2 copy-done.4
  252.2 12.4 %backward.1 = (bf16[4,3,128,768]{3,2,1,0:T(8,128)(2,1)}, f32[1,128]{1,0:T(1,128)}, f32[1,128]{1,0:T(1,128)}) custom-call(bf16[4,3,128,768]{3,2,1,0:T(8,128)(2,1)} %copy-done, s32[512,1]{1,0:T(8,128)} %copy.34.row_ref, s32[1,512]{1,0:T(1,128)} %bitcast.92, f32[1,128]{1,0:T(1,128)} %bitcast.97, f32[1,128]{1,0:T(1,128)} %bitcast.99, ...), custom_call_target="tpu_custom_call" | custom-call | flops 2415919104 | bytes 11010048 | tf_op jit(solution)/shard_map/backward/pallas_call | solution.py:170
  264.6 5.0 %all-to-all-start.6 = ((bf16[4,3,128,768]{3,2,1,0:T(8,128)(2,1)}), bf16[4,3,128,768]{3,2,1,0:T(8,128)(2,1)S(1)}, u32[]{:S(2)}, u32[]{:S(2)}) async-start(bf16[4,3,128,768]{3,2,1,0:T(8,128)(2,1)} %get-tuple-element.10), calls=%async_computation.6 | async-start | bytes 4718592 | tf_op jit(solution)/shard_map/all_to_all | solution.py:182
  269.6 8.6 %forward.1 = bf16[4,128,768]{2,1,0:T(8,128)(2,1)} custom-call(bf16[4,3,128,768]{3,2,1,0:T(8,128)(2,1)} %copy-done, s32[512,1]{1,0:T(8,128)} %copy.34.row_ref, s32[1,512]{1,0:T(1,128)} %bitcast.93, f32[1,128]{1,0:T(1,128)} %bitcast.98, f32[1,128]{1,0:T(1,128)} %bitcast.100), custom_call_target="tpu_custom_call" | custom-call | flops 805306368 | bytes 3145728 | tf_op jit(solution)/shard_map/forward/pallas_call | solution.py:134
  278.3 40.1 %all-to-all-done.6 = bf16[4,3,128,768]{3,2,1,0:T(8,128)(2,1)S(1)} async-done(((bf16[4,3,128,768]{3,2,1,0:T(8,128)(2,1)}), bf16[4,3,128,768]{3,2,1,0:T(8,128)(2,1)S(1)}, u32[]{:S(2)}, u32[]{:S(2)}) %all-to-all-start.6) | async-done | bytes 2359328 | tf_op jit(solution)/shard_map/all_to_all | solution.py:182
  318.4 4.5 broadcast_in_dim.27
  322.9 5.5 %all-to-all-start.7 = ((bf16[8,4,128,768]{3,2,1,0:T(8,128)(2,1)}), bf16[8,4,128,768]{3,2,1,0:T(8,128)(2,1)}, u32[]{:S(2)}, u32[]{:S(2)}) async-start(bf16[8,4,128,768]{3,2,1,0:T(8,128)(2,1)} %broadcast_in_dim.27), calls=%async_computation.7 | async-start | bytes 12582912 | tf_op jit(solution)/shard_map/all_to_all | solution.py:146
  328.4 1.3 slice_bitcast_fusion
  329.7 1.6 copy.37
  331.3 1.2 copy.41
  332.8 1.2 copy.40
  334.4 1.2 copy.39
  335.6 63.7 %all-to-all-done.7 = bf16[8,4,128,768]{3,2,1,0:T(8,128)(2,1)} async-done(((bf16[8,4,128,768]{3,2,1,0:T(8,128)(2,1)}), bf16[8,4,128,768]{3,2,1,0:T(8,128)(2,1)}, u32[]{:S(2)}, u32[]{:S(2)}) %all-to-all-start.7) | async-done | bytes 6291488 | tf_op jit(solution)/shard_map/all_to_all | solution.py:146
  399.2 2.9 fusion.1
  402.1 3.0 fusion.3
  405.1 3.0 fusion.5
  408.2 3.9 multiply_reduce_fusion
  412.8 42.0 %psum.7 = f32[384]{0:T(512)S(1)} all-reduce(f32[384]{0:T(512)S(1)} %pad_maximum_fusion.1), channel_id=1, replica_groups=mesh['dp'=8,'seq'=4] {'dp','seq'}, use_global_device_ids=true, to_apply=%region_3.4 | all-reduce | flops 384 | bytes 3072 | tf_op jit(solution)/shard_map/psum | solution.py:190
  458.5 1.6 broadcast_multiply_fusion
  (47 shorter events, 5.4 us)
Async XLA Ops:
  7.2 84.9 %all-gather.9.cloned.1.call-start = ((), (), s32[]{:S(2)}) async-start(), calls=%async_computation.8 | async-start | bytes 1966080 | tf_op jit(solution)/shard_map/all_gather | solution.py:157
  32.8 1.6 copy-start.5
  33.9 1.2 copy-start.6
  34.4 1.9 copy-start.7
  41.5 102.5 %all-to-all-start = ((bf16[4,3,128,768]{3,2,1,0:T(8,128)(2,1)}), bf16[4,3,128,768]{3,2,1,0:T(8,128)(2,1)S(1)}, u32[]{:S(2)}, u32[]{:S(2)}) async-start(bf16[4,3,128,768]{3,2,1,0:T(8,128)(2,1)} %bitcast.83), calls=%async_computation | async-start | bytes 4718592 | tf_op jit(solution)/shard_map/all_to_all | solution.py:118
  46.8 103.2 %all-gather.11.cloned.1.call-start = ((), (), s32[]{:S(2)}) async-start(), calls=%async_computation.9 | async-start | bytes 1966080 | tf_op jit(solution)/shard_map/all_gather | solution.py:157
  47.6 136.2 %all-gather.13.cloned.1.call-start = ((), (), s32[]{:S(2)}) async-start(), calls=%async_computation.10 | async-start | bytes 1966080 | tf_op jit(solution)/shard_map/all_gather | solution.py:157
  144.1 1.4 copy-start
  145.5 24.2 %all-to-all-start.2 = ((bf16[8,4,32,768]{3,2,1,0:T(8,128)(2,1)}), bf16[8,4,32,768]{3,2,1,0:T(8,128)(2,1)}, u32[]{:S(2)}, u32[]{:S(2)}) async-start(bf16[8,4,32,768]{3,2,1,0:T(8,128)(2,1)} %fusion.7), calls=%async_computation.2 | async-start | bytes 3145728 | tf_op jit(solution)/shard_map/all_to_all | solution.py:161
  169.7 24.5 %all-to-all-start.3 = ((bf16[8,4,32,768]{3,2,1,0:T(8,128)(2,1)}), bf16[8,4,32,768]{3,2,1,0:T(8,128)(2,1)S(1)}, u32[]{:S(2)}, u32[]{:S(2)}) async-start(bf16[8,4,32,768]{3,2,1,0:T(8,128)(2,1)} %fusion.8), calls=%async_computation.3 | async-start | bytes 3145728 | tf_op jit(solution)/shard_map/all_to_all | solution.py:161
  174.7 47.0 %all-gather.15.cloned.1.call-start = ((), (), s32[]{:S(2)}) async-start(), calls=%async_computation.11 | async-start | bytes 1966080 | tf_op jit(solution)/shard_map/all_gather | solution.py:157
  194.2 1.2 copy-start.2
  195.4 30.7 %all-to-all-start.4 = ((bf16[8,4,32,768]{3,2,1,0:T(8,128)(2,1)}), bf16[8,4,32,768]{3,2,1,0:T(8,128)(2,1)S(1)}, u32[]{:S(2)}, u32[]{:S(2)}) async-start(bf16[8,4,32,768]{3,2,1,0:T(8,128)(2,1)} %fusion.9), calls=%async_computation.4 | async-start | bytes 3145728 | tf_op jit(solution)/shard_map/all_to_all | solution.py:161
  226.1 5.4 %copy-start.15 = (s32[1,4]{1,0:T(1,128)S(1)}, s32[1,4]{1,0:T(1,128)}, u32[]{:S(2)}) copy-start(s32[1,4]{1,0:T(1,128)} %param.12) | copy-start | bytes 52
  226.1 1.2 copy-start.3
  227.3 23.7 %all-to-all-start.5 = ((bf16[8,4,32,768]{3,2,1,0:T(8,128)(2,1)}), bf16[8,4,32,768]{3,2,1,0:T(8,128)(2,1)S(1)}, u32[]{:S(2)}, u32[]{:S(2)}) async-start(bf16[8,4,32,768]{3,2,1,0:T(8,128)(2,1)} %fusion.10), calls=%async_computation.5 | async-start | bytes 3145728 | tf_op jit(solution)/shard_map/all_to_all | solution.py:161
  231.7 19.3 %copy-start.8 = (s32[512]{0:T(512)}, s32[512]{0:T(512)S(1)}, u32[]{:S(2)}) copy-start(s32[512]{0:T(512)S(1)} %convert_reduce_fusion) | copy-start | bytes 6148
  251.0 1.2 copy-start.4
  264.6 53.8 %all-to-all-start.6 = ((bf16[4,3,128,768]{3,2,1,0:T(8,128)(2,1)}), bf16[4,3,128,768]{3,2,1,0:T(8,128)(2,1)S(1)}, u32[]{:S(2)}, u32[]{:S(2)}) async-start(bf16[4,3,128,768]{3,2,1,0:T(8,128)(2,1)} %get-tuple-element.10), calls=%async_computation.6 | async-start | bytes 4718592 | tf_op jit(solution)/shard_map/all_to_all | solution.py:182
  322.9 76.4 %all-to-all-start.7 = ((bf16[8,4,128,768]{3,2,1,0:T(8,128)(2,1)}), bf16[8,4,128,768]{3,2,1,0:T(8,128)(2,1)}, u32[]{:S(2)}, u32[]{:S(2)}) async-start(bf16[8,4,128,768]{3,2,1,0:T(8,128)(2,1)} %broadcast_in_dim.27), calls=%async_computation.7 | async-start | bytes 12582912 | tf_op jit(solution)/shard_map/all_to_all | solution.py:146
  329.7 2.8 copy-start.1
  334.0 65.2 %copy-start.13 = (bf16[8,128,768]{2,1,0:T(8,128)(2,1)S(1)}, bf16[8,128,768]{2,1,0:T(8,128)(2,1)}, u32[]{:S(2)}) copy-start(bf16[8,128,768]{2,1,0:T(8,128)(2,1)} %all-gather.13.cloned.1.call-done) | copy-start | bytes 4718596
  335.6 66.6 %copy-start.12 = (bf16[8,128,768]{2,1,0:T(8,128)(2,1)S(1)}, bf16[8,128,768]{2,1,0:T(8,128)(2,1)}, u32[]{:S(2)}) copy-start(bf16[8,128,768]{2,1,0:T(8,128)(2,1)} %all-gather.11.cloned.1.call-done) | copy-start | bytes 4718596
  402.1 3.0 copy-start.11
  405.1 3.0 copy-start.14
  408.2 4.6 copy-start.9
  408.2 4.6 copy-start.10
Sparse Core Ops, SparseCore 0:
  34.1 57.8 all-gather.8
  93.6 50.1 all-gather.10
  145.4 38.2 all-gather.12
  185.8 35.8 all-gather.14

commit v2 on v1

v2 whole, which is shorter than its diff:
```python
import functools

import jax
import jax.numpy as jnp
from jax import lax
from jax.experimental import pallas as pl
from jax.experimental.pallas import tpu as pltpu
from jax.sharding import PartitionSpec as P

HEAD_DIM = 128
MAX_NORM = 768
EPS = 1e-06
SCALE = HEAD_DIM ** (-0.5)
NT = (((1,), (1,)), ((), ()))
TN = (((0,), (0,)), ((), ()))
NN = (((1,), (0,)), ((), ()))


def mm(a, b, dims):
    return lax.dot_general(a, b, dims, preferred_element_type=jnp.float32)


def segment_ids(lengths, total):
    ends = jnp.cumsum(lengths)
    places = jnp.arange(total, dtype=jnp.int32)
    return jnp.sum((places[:, None] >= ends[None, :]).astype(jnp.int32), axis=1)


def unit_rows(rows):
    wide = rows.astype(jnp.float32)
    inverse = lax.rsqrt(jnp.mean(wide * wide, axis=-1, keepdims=True) + EPS)
    return wide * inverse, inverse


def probs_of(qn, kn, same):
    scores = mm(qn, kn, NT) * SCALE
    expo = jnp.where(same, jnp.exp(scores), 0.0)
    return (expo * (1.0 / jnp.sum(expo, axis=-1, keepdims=True))).astype(jnp.bfloat16)


def forward_kernel(q_ref, k_ref, v_ref, row_ref, col_ref, qg_ref, kg_ref, out_ref):
    qn = (unit_rows(q_ref[...])[0] * qg_ref[...]).astype(jnp.bfloat16)
    kn = (unit_rows(k_ref[...])[0] * kg_ref[...]).astype(jnp.bfloat16)
    probs = probs_of(qn, kn, row_ref[...] == col_ref[...])
    out_ref[...] = mm(probs, v_ref[...], NN).astype(jnp.bfloat16)


def norm_back(unit, inverse, gain, d_norm):
    part = jnp.sum(unit * d_norm, axis=0, keepdims=True)
    d_unit = d_norm * gain
    d_rows = inverse * (d_unit - unit * jnp.mean(unit * d_unit, axis=-1, keepdims=True))
    return d_rows.astype(jnp.bfloat16), part


def backward_kernel(
    q_ref, k_ref, v_ref, row_ref, col_ref, qg_ref, kg_ref, d_ref,
    dq_ref, dk_ref, dv_ref, qpart_ref, kpart_ref,
):
    q_unit, q_inv = unit_rows(q_ref[...])
    k_unit, k_inv = unit_rows(k_ref[...])
    qg, kg = qg_ref[...], kg_ref[...]
    qn = (q_unit * qg).astype(jnp.bfloat16)
    kn = (k_unit * kg).astype(jnp.bfloat16)
    probs = probs_of(qn, kn, row_ref[...] == col_ref[...])
    d_attn = d_ref[...]
    d_probs = mm(d_attn, v_ref[...], NT)
    probs32 = probs.astype(jnp.float32)
    row_sum = jnp.sum(probs32 * d_probs, axis=-1, keepdims=True)
    d_scores = (probs32 * (d_probs - row_sum) * SCALE).astype(jnp.bfloat16)
    dv_ref[...] = mm(probs, d_attn, TN).astype(jnp.bfloat16)
    dq_ref[...], qpart = norm_back(q_unit, q_inv, qg, mm(d_scores, kn, NN))
    dk_ref[...], kpart = norm_back(k_unit, k_inv, kg, mm(d_scores, qn, TN))

    @pl.when(pl.program_id(0) == 0)
    def _():
        qpart_ref[...] = jnp.zeros_like(qpart_ref)
        kpart_ref[...] = jnp.zeros_like(kpart_ref)

    qpart_ref[...] += qpart
    kpart_ref[...] += kpart


def sum_kernel(axis, size, x_ref, out_ref, held, send_sem, recv_sem):
    me = lax.axis_index(axis)
    peers = [lax.rem(me + step, size) for step in range(1, size)]
    barrier = pltpu.get_barrier_semaphore()
    for peer in peers:
        pl.semaphore_signal(
            barrier, inc=1, device_id={axis: peer}, device_id_type=pl.DeviceIdType.MESH
        )
    pl.semaphore_wait(barrier, size - 1)
    copies = [
        pltpu.make_async_remote_copy(
            src_ref=x_ref,
            dst_ref=held.at[me],
            send_sem=send_sem.at[step],
            recv_sem=recv_sem.at[step],
            device_id={axis: peer},
            device_id_type=pl.DeviceIdType.MESH,
        )
        for step, peer in enumerate(peers)
    ]
    for copy in copies:
        copy.start()
    held[me] = x_ref[...]
    for copy in copies:
        copy.wait()
    total = held[0]
    for source in range(1, size):
        total = total + held[source]
    out_ref[...] = total


def sum_over(x, axis, size, collective_id):
    return pl.pallas_call(
        functools.partial(sum_kernel, axis, size),
        in_specs=[pl.BlockSpec(memory_space=pltpu.VMEM)],
        out_specs=pl.BlockSpec(memory_space=pltpu.VMEM),
        out_shape=jax.ShapeDtypeStruct(x.shape, x.dtype),
        scratch_shapes=[
            pltpu.VMEM((size,) + x.shape, x.dtype),
            pltpu.SemaphoreType.DMA((size - 1,)),
            pltpu.SemaphoreType.DMA((size - 1,)),
        ],
        compiler_params=pltpu.CompilerParams(
            collective_id=collective_id, has_side_effects=True
        ),
        name="sum_" + axis,
    )(x)


def local(
    query_rows, key_rows, value_rows, out_grad, clip_lengths, out_weight, query_gain, key_gain,
    n, groups,
):
    rows, inner = query_rows.shape[1:]
    width = inner // n
    heads = width // HEAD_DIM
    total = n * rows

    qkv = [
        lax.all_to_all(x[0], "seq", split_axis=1, concat_axis=0, tiled=True)
        for x in (query_rows, key_rows, value_rows)
    ]
    out_full = lax.all_gather(out_grad[0], "seq", axis=0, tiled=True)
    seg = segment_ids(clip_lengths[0], total)
    shared = [seg[:, None], seg[None, :], query_gain[None], key_gain[None]]
    head = pl.BlockSpec((total, HEAD_DIM), lambda h: (0, h))
    one = pl.BlockSpec((1, HEAD_DIM), lambda h: (0, 0))
    small = [
        pl.BlockSpec((total, 1), lambda h: (0, 0)),
        pl.BlockSpec((1, total), lambda h: (0, 0)),
        one,
        one,
    ]
    params = pltpu.CompilerParams(
        dimension_semantics=("arbitrary",), vmem_limit_bytes=60 * 1024 * 1024
    )
    square = total * total * heads
    flat = jax.ShapeDtypeStruct((total, width), jnp.bfloat16)
    attn = pl.pallas_call(
        forward_kernel,
        grid=(heads,),
        in_specs=[head] * 3 + small,
        out_specs=head,
        out_shape=flat,
        compiler_params=params,
        cost_estimate=pl.CostEstimate(
            flops=4 * square * HEAD_DIM, bytes_accessed=8 * total * width, transcendentals=square
        ),
        name="forward",
    )(*qkv, *shared)
    weight_part = lax.dot_general(attn, out_full, TN, preferred_element_type=jnp.float32)
    weight_shard = lax.psum_scatter(
        weight_part.astype(jnp.bfloat16), "dp", scatter_dimension=1, tiled=True
    ).astype(jnp.float32)
    d_attn = mm(out_full, out_weight, NT).astype(jnp.bfloat16)
    row = jax.ShapeDtypeStruct((1, HEAD_DIM), jnp.float32)
    *grads, qpart, kpart = pl.pallas_call(
        backward_kernel,
        grid=(heads,),
        in_specs=[head] * 3 + small + [head],
        out_specs=(head, head, head, one, one),
        out_shape=(flat, flat, flat, row, row),
        compiler_params=params,
        cost_estimate=pl.CostEstimate(
            flops=12 * square * HEAD_DIM, bytes_accessed=14 * total * width, transcendentals=square
        ),
        name="backward",
    )(*qkv, *shared, d_attn)
    query_back, key_back, value_back = (
        lax.all_to_all(x, "seq", split_axis=0, concat_axis=1, tiled=True)[None] for x in grads
    )

    level = jnp.full((6, HEAD_DIM), jnp.sum(weight_shard * weight_shard))
    packed = jnp.concatenate([qpart, kpart, level])
    packed = sum_over(sum_over(packed, "dp", groups, 0), "seq", n, 1)
    qgain_raw, kgain_raw = packed[0], packed[1]
    squares = packed[2, 0] + jnp.sum(qgain_raw * qgain_raw) + jnp.sum(kgain_raw * kgain_raw)
    grad_norm = jnp.sqrt(squares)
    factor = jnp.minimum(jnp.float32(1.0), MAX_NORM / (grad_norm + EPS))
    return (
        query_back,
        key_back,
        value_back,
        weight_shard * factor,
        qgain_raw * factor,
        kgain_raw * factor,
        grad_norm,
    )


def solution(mesh):
    rows = P("dp", "seq", None)
    return jax.shard_map(
        functools.partial(local, n=mesh.shape["seq"], groups=mesh.shape["dp"]),
        mesh=mesh,
        in_specs=(rows, rows, rows, rows, P("dp", None), P("seq", None), P(), P()),
        out_specs=(rows, rows, rows, P("seq", "dp"), P(), P(), P()),
        check_vma=False,
    )
```

time: 469 us -> 311 us (0.66)
  waiting for transfers between devices: 267 us -> 136 us
  blocking collectives: 65.6 us -> 49 us
  Pallas kernels: 21 us -> 35.5 us
  local copies, waits for them, and re-layouts: 27.8 us -> 15.9 us
  matrix products: 30.3 us -> 20.3 us
  starting transfers between devices: 34.8 us -> 25.3 us
    all_to_all x7 -> x4, waiting for transfers between devices: 191 us -> 120 us  [the longest x3 108 us: local(): lax.all_to_all(x[0], 'seq', split_axis=1, concat_axis=0, tiled=True)]
    all_gather x4 -> x1, waiting for transfers between devices: 73.5 us -> 15.3 us  [local(): out_full = lax.all_gather(out_grad[0], 'seq', axis=0, tiled=True)]
    psum x1 -> x0, blocking collectives: 42 us -> none  [local(): packed = lax.psum(packed, ('dp', 'seq'))]
    all_to_all x1 -> x2, blocking collectives: 23.5 us -> 49 us  [local(): lax.all_to_all(x, 'seq', split_axis=0, concat_axis=1, tiled=True)[None]]
    pallas_call x2 -> x4, Pallas kernels: 21 us -> 35.5 us  [the longest x2 14.7 us: sum_over(): pl.pallas_call(functools.partial(sum_kernel, axis, size), in_specs=[pl.Bl...]
    unnamed x39 -> x18, local copies, waits for them, and re-layouts: 13.8 us -> 0.9 us
    dot_general x8 -> x2, matrix products: 30.3 us -> 20.3 us  [the longest x1 10.7 us: mm(): return lax.dot_general(a, b, dims, preferred_element_type=jnp.float32)]
    all_to_all x7 -> x4, starting transfers between devices: 34.7 us -> 25.3 us  [the longest x3 19.9 us: local(): lax.all_to_all(x[0], 'seq', split_axis=1, concat_axis=0, tiled=True)]
  transfers between devices with their start and end apart: 11 -> 6, of which waited for: 9 -> 5; matrix products, arithmetic and copies ran while one was open for 7% -> 7% of each run, Pallas kernels for 2% -> 7%
where the time goes in v2:
time: 311 us; the launch traced here: 308 us
  waiting for transfers between devices  136 us (44%)
  blocking collectives  49 us (16%)
  Pallas kernels  35.5 us (11%)
  starting transfers between devices  25.3 us (8%)
  matrix products  20.3 us (7%)
  between operations  17.3 us (6%)
  local copies, waits for them, and re-layouts  15.9 us (5%)
  other arithmetic  8.86 us (3%)
    all_to_all x3, waiting for transfers between devices, local(): lax.all_to_all(x[0], 'seq', split_axis=1, concat_axis=0, tiled=True)  108 us
    all_to_all x2, blocking collectives, local(): lax.all_to_all(x, 'seq', split_axis=0, concat_axis=1, tiled=True)[None]  49 us
    all_to_all x3, starting transfers between devices, local(): lax.all_to_all(x[0], 'seq', split_axis=1, concat_axis=0, tiled=True)  19.9 us
    all_gather x1, waiting for transfers between devices, local(): out_full = lax.all_gather(out_grad[0], 'seq', axis=0, tiled=True)  15.3 us
    pallas_call x2, Pallas kernels, sum_over(): pl.pallas_call(functools.partial(sum_kernel, axis, size), in_specs=[pl.Bl...  14.7 us
    pallas_call x1, Pallas kernels, local(): pl.pallas_call(backward_kernel, grid=(heads,), in_specs=[head] * 3 + smal...  12 us
    all_to_all x1, waiting for transfers between devices, local(): lax.all_to_all(x, 'seq', split_axis=0, concat_axis=1, tiled=True)[None]  11.8 us
    dot_general x1, matrix products, mm(): return lax.dot_general(a, b, dims, preferred_element_type=jnp.float32)  10.7 us
  transfers between devices with their start and end apart: 6, of which 5 were waited for; matrix products, arithmetic and copies ran while one was open for 7% of the time, Pallas kernels for 7%

profile of v2, /device:TPU:12, one launch (start us, length us, event | category | flops | bytes accessed | tf_op | source)
XLA Modules:
  0.0 308.0 jit_solution(3188471251215611718)
XLA Ops:
  7.2 0.0 copy-start.3
  7.2 0.0 all-gather.3.cloned.1.call-start
  7.2 0.7 all-gather.3.cloned.1.call-update
  7.9 2.0 all_to_all.78
  9.9 0.0 copy-start.8
  9.9 1.0 copy.29
  10.9 5.3 %all-to-all-start = ((bf16[128,4,768]{2,0,1:T(8,128)(2,1)}), bf16[128,4,768]{2,0,1:T(8,128)(2,1)S(1)}, u32[]{:S(2)}, u32[]{:S(2)}) async-start(bf16[128,4,768]{2,0,1:T(8,128)(2,1)} %copy.29), calls=%async_computation | async-start | bytes 1572864 | tf_op jit(solution)/shard_map/all_to_all | solution.py:142
  16.2 0.6 all_to_all.82
  16.8 1.0 copy.30
  17.7 34.1 %all-to-all-done = bf16[128,4,768]{2,0,1:T(8,128)(2,1)S(1)} async-done(((bf16[128,4,768]{2,0,1:T(8,128)(2,1)}), bf16[128,4,768]{2,0,1:T(8,128)(2,1)S(1)}, u32[]{:S(2)}, u32[]{:S(2)}) %all-to-all-start) | async-done | bytes 786464 | tf_op jit(solution)/shard_map/all_to_all | solution.py:142
  51.9 8.5 %all-to-all-start.1 = ((bf16[128,4,768]{2,0,1:T(8,128)(2,1)}), bf16[128,4,768]{2,0,1:T(8,128)(2,1)S(1)}, u32[]{:S(2)}, u32[]{:S(2)}) async-start(bf16[128,4,768]{2,0,1:T(8,128)(2,1)} %copy.30), calls=%async_computation.1 | async-start | bytes 1572864 | tf_op jit(solution)/shard_map/all_to_all | solution.py:142
  60.4 0.6 all_to_all.86
  60.9 1.0 copy.31
  61.9 36.2 %all-to-all-done.1 = bf16[128,4,768]{2,0,1:T(8,128)(2,1)S(1)} async-done(((bf16[128,4,768]{2,0,1:T(8,128)(2,1)}), bf16[128,4,768]{2,0,1:T(8,128)(2,1)S(1)}, u32[]{:S(2)}, u32[]{:S(2)}) %all-to-all-start.1) | async-done | bytes 786464 | tf_op jit(solution)/shard_map/all_to_all | solution.py:142
  98.1 6.1 %all-to-all-start.2 = ((bf16[128,4,768]{2,0,1:T(8,128)(2,1)}), bf16[128,4,768]{2,0,1:T(8,128)(2,1)S(1)}, u32[]{:S(2)}, u32[]{:S(2)}) async-start(bf16[128,4,768]{2,0,1:T(8,128)(2,1)} %copy.31), calls=%async_computation.2 | async-start | bytes 1572864 | tf_op jit(solution)/shard_map/all_to_all | solution.py:142
  104.2 0.0 reduce-scatter.2.cloned.1.call-start
  104.2 0.2 reduce-window.8
  104.4 0.1 convert_reduce_fusion
  104.5 0.9 copy.32.row_ref
  105.3 37.8 %all-to-all-done.2 = bf16[128,4,768]{2,0,1:T(8,128)(2,1)S(1)} async-done(((bf16[128,4,768]{2,0,1:T(8,128)(2,1)}), bf16[128,4,768]{2,0,1:T(8,128)(2,1)S(1)}, u32[]{:S(2)}, u32[]{:S(2)}) %all-to-all-start.2) | async-done | bytes 786464 | tf_op jit(solution)/shard_map/all_to_all | solution.py:142
  143.1 0.9 copy-done.2
  143.9 8.8 %forward.1 = bf16[512,768]{1,0:T(8,128)(2,1)} custom-call(bf16[512,768]{1,0:T(8,128)(2,1)} %bitcast.38, bf16[512,768]{1,0:T(8,128)(2,1)} %bitcast.40, bf16[512,768]{1,0:T(8,128)(2,1)} %bitcast.42, s32[512,1]{1,0:T(8,128)} %copy.32.row_ref, s32[1,512]{1,0:T(1,128)} %bitcast.48, f32[1,128]{1,0:T(1,128)} %bitcast.51, f32[1,128]{1,0:T(1,128)} %bitcast.53), custom_call_target="tpu_custom_call" | custom-call | flops 805306368 | bytes 3145728 | tf_op jit(solution)/shard_map/forward/pallas_call | solution.py:161
  152.8 15.3 %all-gather.3.cloned.1.call-done = bf16[1,512,6144]{2,1,0:T(8,128)(2,1)} async-done(((bf16[1,128,6144]{2,1,0:T(8,128)(2,1)}), bf16[1,512,6144]{2,1,0:T(8,128)(2,1)}) %all-gather.3.cloned.1.call-update) | async-done | bytes 6291472 | tf_op jit(solution)/shard_map/all_gather | solution.py:145
  168.1 9.6 %convolution_convert_fusion = bf16[768,6144]{1,0:T(8,128)(2,1)} fusion(bf16[512,768]{1,0:T(8,128)(2,1)} %forward.1, bf16[1,512,6144]{2,1,0:T(8,128)(2,1)} %all-gather.3.cloned.1.call-done), kind=kOutput, calls=%fused_computation | convolution fusion | flops 4836556800 | bytes 16515072 | tf_op jit(solution)/shard_map/dot_general | solution.py:173
  177.7 0.0 reduce-scatter.2.cloned.1.call-update
  177.7 10.7 %fusion.4.d_ref = bf16[512,768]{1,0:T(8,128)(2,1)} fusion(bf16[768,6144]{1,0:T(8,128)(2,1)} %param.13, bf16[1,512,6144]{2,1,0:T(8,128)(2,1)} %all-gather.3.cloned.1.call-done), kind=kOutput, calls=%fused_computation.7 | convolution fusion | flops 4832231424 | bytes 16515072 | tf_op jit(solution)/shard_map/dot_general | solution.py:20
  188.4 12.0 %backward.1 = (bf16[512,768]{1,0:T(8,128)(2,1)}, bf16[512,768]{1,0:T(8,128)(2,1)}, bf16[512,768]{1,0:T(8,128)(2,1)}, f32[1,128]{1,0:T(1,128)}, f32[1,128]{1,0:T(1,128)}) custom-call(bf16[512,768]{1,0:T(8,128)(2,1)} %bitcast.39, bf16[512,768]{1,0:T(8,128)(2,1)} %bitcast.41, bf16[512,768]{1,0:T(8,128)(2,1)} %bitcast.43, s32[512,1]{1,0:T(8,128)} %copy.32.row_ref, ...), custom_call_target="tpu_custom_call" | custom-call | flops 2415919104 | bytes 5505024 | tf_op jit(solution)/shard_map/backward/pallas_call | solution.py:179
  200.5 25.8 %all_to_all.105 = bf16[4,128,768]{2,1,0:T(8,128)(2,1)S(1)} all-to-all(bf16[4,128,768]{2,1,0:T(8,128)(2,1)} %bitcast.46), channel_id=1, replica_groups=mesh['dp'=8,'seq'=4] {'seq'}, dimensions={0} | all-to-all | bytes 1572864 | tf_op jit(solution)/shard_map/all_to_all | solution.py:192
  226.3 23.2 %all_to_all.106 = bf16[4,128,768]{2,1,0:T(8,128)(2,1)S(1)} all-to-all(bf16[4,128,768]{2,1,0:T(8,128)(2,1)} %bitcast.45), channel_id=1, replica_groups=mesh['dp'=8,'seq'=4] {'seq'}, dimensions={0} | all-to-all | bytes 1572864 | tf_op jit(solution)/shard_map/all_to_all | solution.py:192
  249.4 5.4 %all-to-all-start.5 = ((bf16[4,128,768]{2,1,0:T(8,128)(2,1)}), bf16[4,128,768]{2,1,0:T(8,128)(2,1)S(1)}, u32[]{:S(2)}, u32[]{:S(2)}) async-start(bf16[4,128,768]{2,1,0:T(8,128)(2,1)} %bitcast.44), calls=%async_computation.5 | async-start | bytes 1572864 | tf_op jit(solution)/shard_map/all_to_all | solution.py:192
  254.9 0.6 copy.34
  255.5 1.5 broadcast_in_dim.31
  256.9 0.6 copy.33
  257.5 1.5 broadcast_in_dim.30
  259.0 11.8 %all-to-all-done.5 = bf16[4,128,768]{2,1,0:T(8,128)(2,1)S(1)} async-done(((bf16[4,128,768]{2,1,0:T(8,128)(2,1)}), bf16[4,128,768]{2,1,0:T(8,128)(2,1)S(1)}, u32[]{:S(2)}, u32[]{:S(2)}) %all-to-all-start.5) | async-done | bytes 786464 | tf_op jit(solution)/shard_map/all_to_all | solution.py:192
  270.7 0.6 copy.35
  271.4 1.5 broadcast_in_dim.32
  272.8 2.5 fusion.3
  275.3 0.6 broadcast_in_dim.33
  275.9 0.1 pad.2.clone
  276.0 0.0 copy-done.7
  276.0 0.7 maximum_maximum_fusion.x_ref
  276.7 6.1 %sum_dp.1.x_ref = f32[8,128]{1,0:T(8,128)} custom-call(f32[8,128]{1,0:T(8,128)} %maximum_maximum_fusion.x_ref), custom_call_target="tpu_custom_call" | custom-call | tf_op jit(solution)/shard_map/sum_dp/pallas_call | solution.py:115
  282.8 8.6 %sum_seq.1 = f32[8,128]{1,0:T(8,128)} custom-call(f32[8,128]{1,0:T(8,128)} %sum_dp.1.x_ref), custom_call_target="tpu_custom_call" | custom-call | tf_op jit(solution)/shard_map/sum_seq/pallas_call | solution.py:115
  291.4 1.2 slice.9
  292.6 1.4 multiply_reduce_fusion
  295.9 1.3 multiply_bitcast_fusion
  297.2 2.8 convert_multiply_fusion
  (15 shorter events, 0.0 us)
Async XLA Ops:
  7.2 9.0 %copy-start.3 = (bf16[1,128,3072]{2,1,0:T(8,128)(2,1)S(1)}, bf16[1,128,3072]{2,1,0:T(8,128)(2,1)}, u32[]{:S(2)}) copy-start(bf16[1,128,3072]{2,1,0:T(8,128)(2,1)} %param.9) | copy-start | bytes 2359300
  7.2 53.2 %copy-start.4 = (bf16[1,128,3072]{2,1,0:T(8,128)(2,1)S(1)}, bf16[1,128,3072]{2,1,0:T(8,128)(2,1)}, u32[]{:S(2)}) copy-start(bf16[1,128,3072]{2,1,0:T(8,128)(2,1)} %param.10) | copy-start | bytes 2359300
  7.2 160.9 %all-gather.3.cloned.1.call-start = ((), (), s32[]{:S(2)}) async-start(), calls=%async_computation.8 | async-start | bytes 7864320 | tf_op jit(solution)/shard_map/all_gather | solution.py:145
  9.9 94.3 %copy-start.8 = (s32[1,4]{1,0:T(1,128)S(1)}, s32[1,4]{1,0:T(1,128)}, u32[]{:S(2)}) copy-start(s32[1,4]{1,0:T(1,128)} %param.12) | copy-start | bytes 52
  10.9 41.0 %all-to-all-start = ((bf16[128,4,768]{2,0,1:T(8,128)(2,1)}), bf16[128,4,768]{2,0,1:T(8,128)(2,1)S(1)}, u32[]{:S(2)}, u32[]{:S(2)}) async-start(bf16[128,4,768]{2,0,1:T(8,128)(2,1)} %copy.29), calls=%async_computation | async-start | bytes 1572864 | tf_op jit(solution)/shard_map/all_to_all | solution.py:142
  51.9 91.2 %copy-start = (bf16[128,4,768]{2,0,1:T(8,128)(2,1)}, bf16[128,4,768]{2,0,1:T(8,128)(2,1)S(1)}, u32[]{:S(2)}) copy-start(bf16[128,4,768]{2,0,1:T(8,128)(2,1)S(1)} %all-to-all-done) | copy-start | bytes 2359300
  51.9 46.3 %all-to-all-start.1 = ((bf16[128,4,768]{2,0,1:T(8,128)(2,1)}), bf16[128,4,768]{2,0,1:T(8,128)(2,1)S(1)}, u32[]{:S(2)}, u32[]{:S(2)}) async-start(bf16[128,4,768]{2,0,1:T(8,128)(2,1)} %copy.30), calls=%async_computation.1 | async-start | bytes 1572864 | tf_op jit(solution)/shard_map/all_to_all | solution.py:142
  98.1 44.9 %copy-start.1 = (bf16[128,4,768]{2,0,1:T(8,128)(2,1)}, bf16[128,4,768]{2,0,1:T(8,128)(2,1)S(1)}, u32[]{:S(2)}) copy-start(bf16[128,4,768]{2,0,1:T(8,128)(2,1)S(1)} %all-to-all-done.1) | copy-start | bytes 2359300
  98.1 44.9 %all-to-all-start.2 = ((bf16[128,4,768]{2,0,1:T(8,128)(2,1)}), bf16[128,4,768]{2,0,1:T(8,128)(2,1)S(1)}, u32[]{:S(2)}, u32[]{:S(2)}) async-start(bf16[128,4,768]{2,0,1:T(8,128)(2,1)} %copy.31), calls=%async_computation.2 | async-start | bytes 1572864 | tf_op jit(solution)/shard_map/all_to_all | solution.py:142
  104.2 168.6 %reduce-scatter.2.cloned.1.call-start = ((), (), s32[]{:S(2)}) async-start(), calls=%async_computation.7 | async-start | bytes 10616832 | tf_op jit(solution)/shard_map/reduce_scatter | solution.py:174
  104.5 38.6 %copy-start.5 = (s32[512]{0:T(512)}, s32[512]{0:T(512)S(1)}, u32[]{:S(2)}) copy-start(s32[512]{0:T(512)S(1)} %convert_reduce_fusion) | copy-start | bytes 6148
  143.1 0.9 copy-start.2
  249.4 26.6 %copy-start.6 = (f32[1,128]{1,0:T(1,128)S(1)}, f32[1,128]{1,0:T(1,128)}, u32[]{:S(2)}) copy-start(f32[1,128]{1,0:T(1,128)} %get-tuple-element.15) | copy-start | bytes 1540
  249.4 26.6 %copy-start.7 = (f32[1,128]{1,0:T(1,128)S(1)}, f32[1,128]{1,0:T(1,128)}, u32[]{:S(2)}) copy-start(f32[1,128]{1,0:T(1,128)} %get-tuple-element.16) | copy-start | bytes 1540
  249.4 21.3 %all-to-all-start.5 = ((bf16[4,128,768]{2,1,0:T(8,128)(2,1)}), bf16[4,128,768]{2,1,0:T(8,128)(2,1)S(1)}, u32[]{:S(2)}, u32[]{:S(2)}) async-start(bf16[4,128,768]{2,1,0:T(8,128)(2,1)} %bitcast.44), calls=%async_computation.5 | async-start | bytes 1572864 | tf_op jit(solution)/shard_map/all_to_all | solution.py:192
Sparse Core Ops, SparseCore 0:
  9.6 158.4 all-gather.2
  177.9 78.6 reduce-scatter.1
